TPU v7x, 256 devices: a whole 4x4x8 slice. The times are simulated.
256 devices in a mesh: lat: 8 (over x, core), lon: 32 (over y, z).
Axes of the slice: x: 4, y: 4, z: 8, core: 2. Of those that a mesh axis runs over, the one named last changes fastest.
Arguments:
- prediction_fields: float32 [4, 69, 1440, 1024], P(None, None, 'lon', 'lat'), may hold values from -16 to 16
- verifying_state: float32 [69, 1440, 1024], P(None, 'lon', 'lat'), may hold values from -16 to 16
- normal_state: float32 [69, 1440, 1024], P(None, 'lon', 'lat'), may hold values from -16 to 16
- evaluated_point_flag: int32 [1440, 1024], P('lon', 'lat'), may hold values 0 or 1
- parallels_each_strip: int32 [8], replicated, may hold values from 1 to 128, 721 in all
Outputs:
- parallel_quadratic_error: float32 [4, 69, 1024], P(None, None, 'lat')
- parallel_systematic_error: float32 [4, 69, 1024], P(None, None, 'lat')
- parallel_pattern_skill: float32 [4, 69, 1024], P(None, None, 'lat')
- rmse: float32 [4, 69], replicated
- systematic_error: float32 [4, 69], replicated
- pattern_skill: float32 [4, 69], replicated
Inputs may be any that keep to these rules, and one draw needn't show every extreme that they name: `parallels_each_strip`: they sum to 721, and some band holds exactly 128 rows.
All inputs are finite; a program needn't handle non-finite values.
Results may differ from a plain program's by a relative error of at most 0.00002.
Values sent between devices are 32-bit elements.
A program may use at most 64 MiB of HBM per device.

v0:
```python
import functools
import jax
import jax.numpy as jnp
from jax import lax
from jax.sharding import Mesh
from jax.sharding import PartitionSpec as P

MEAN_ROWS = 90
LAT = ("lat_0", "lat_1")
LON = ("lon_0", "lon_1")
LAT_LON = ("lat_0", "lat_1", "lon_0", "lon_1")
minimum_divisor = 0.1


def by_axis(shard, axes):
    return functools.reduce(lax.psum, axes, shard)


def split_up(shard, dim, devices):
    dims = shard.shape
    tiles = shard.reshape(*dims[:dim], devices, dims[dim] // devices, *dims[dim + 1 :])
    return jnp.moveaxis(tiles, dim, 0)


def sent_and_summed(shard, axis, dim):
    devices = lax.axis_size(axis)
    tiles = lax.all_to_all(split_up(shard, dim, devices), axis, 0, 0, tiled=True)
    return jnp.sum(tiles, axis=0)


def gather_turned(arrays, axis, dims):
    turned = [jnp.moveaxis(a, dim, 0) for a, dim in zip(arrays, dims)]
    both = jnp.concatenate([t.reshape(len(t), -1) for t in turned], axis=1)
    filled, at, done = (lax.all_gather(both, axis, axis=0, tiled=True), 0, [])
    for t, dim in zip(turned, dims):
        slab = filled[:, at : at + t[0].size].reshape(-1, *t.shape[1:])
        done.append(jnp.moveaxis(slab, 0, dim))
        at += t[0].size
    return tuple(done)


def stacked_metrics(totals, horizon_tally, quantity_tally, grid_point_tally):
    block_rows = horizon_tally * quantity_tally
    width = totals.shape[1]
    error_power_two = (
        totals[:block_rows].reshape(horizon_tally, quantity_tally, width) / grid_point_tally
    )
    prediction_error = (
        totals[block_rows : 2 * block_rows].reshape(horizon_tally, quantity_tally, width)
        / grid_point_tally
    )
    paired_anomaly_term = (
        totals[2 * block_rows : 3 * block_rows].reshape(horizon_tally, quantity_tally, width)
        / grid_point_tally
    )
    predicted_spread_sum = (
        totals[3 * block_rows : 4 * block_rows].reshape(horizon_tally, quantity_tally, width)
        / grid_point_tally
    )
    observed_dispersion = (
        totals[4 * block_rows :].reshape(1, quantity_tally, width) / grid_point_tally
    )
    divisor_term = jnp.sqrt(
        jnp.maximum(predicted_spread_sum, minimum_divisor)
        * jnp.maximum(observed_dispersion, minimum_divisor)
    )
    return (error_power_two, prediction_error, paired_anomaly_term / divisor_term)


def local(
    prediction_fields, verifying_state, normal_state, evaluated_point_flag, parallels_each_strip
):
    horizon_tally, quantity_tally, zonal_circle_size, parallel_index = prediction_fields.shape
    lat_bands = lax.axis_size(LAT)
    lon_spokes = lax.axis_size(LON)
    lat_total = MEAN_ROWS * lat_bands + 1
    lon_total = zonal_circle_size * lon_spokes
    band_index = lax.axis_index(LAT)
    band_ids = jnp.arange(lat_bands, dtype=jnp.int32)
    first_row = jnp.sum(jnp.where(band_ids < band_index, parallels_each_strip, 0))
    band_filled = jnp.sum(jnp.where(band_ids == band_index, parallels_each_strip, 0))
    slot_ids = jnp.arange(parallel_index, dtype=jnp.int32)
    inside_band = slot_ids < band_filled
    angles = jnp.pi * jnp.arange(lat_total, dtype=jnp.float32) / (lat_total - 1)
    normalizer = jnp.sum(jnp.sin(angles))
    row_angle = jnp.pi * (first_row + slot_ids).astype(jnp.float32) / (lat_total - 1)
    area_factors = jnp.where(inside_band, jnp.sin(row_angle) * lat_total / normalizer, 0.0)
    retain_filter = (
        evaluated_point_flag.astype(jnp.float32) * inside_band.astype(jnp.float32)[None, :]
    )
    observed_anomaly = verifying_state - normal_state
    predicted_anomaly = prediction_fields - normal_state[None]
    mistake_field = predicted_anomaly - observed_anomaly[None]
    retained_entries = retain_filter[None, None]
    block_rows = horizon_tally * quantity_tally
    partial_value = jnp.concatenate(
        [
            jnp.sum(retained_entries * mistake_field * mistake_field, axis=2).reshape(
                block_rows, parallel_index
            ),
            jnp.sum(retained_entries * mistake_field, axis=2).reshape(block_rows, parallel_index),
            jnp.sum(retained_entries * predicted_anomaly * observed_anomaly[None], axis=2).reshape(
                block_rows, parallel_index
            ),
            jnp.sum(retained_entries * predicted_anomaly * predicted_anomaly, axis=2).reshape(
                block_rows, parallel_index
            ),
            jnp.sum(retain_filter[None] * observed_anomaly * observed_anomaly, axis=1),
        ],
        axis=0,
    )
    grand = by_axis(jnp.sum(partial_value * area_factors, axis=1), LAT_LON)
    shares = sent_and_summed(partial_value, LON, 1)
    scores = stacked_metrics(shares, horizon_tally, quantity_tally, float(lon_total))
    error_power_two, prediction_error, covariance_sum = gather_turned(
        (scores[0], scores[1], scores[2]), LON, (2, 2, 2)
    )
    total_square, total_offset, total_agree = stacked_metrics(
        grand[:, None], horizon_tally, quantity_tally, float(lat_total * lon_total)
    )
    rmse = jnp.sqrt(jnp.maximum(total_square[:, :, 0], minimum_divisor))
    return (
        error_power_two,
        prediction_error,
        covariance_sum,
        rmse,
        total_offset[:, :, 0],
        total_agree[:, :, 0],
    )


def solution(mesh):
    split = Mesh(mesh.devices.reshape(4, 2, 4, 8), ("lat_0", "lat_1", "lon_0", "lon_1"))
    placed = (P(None, None, LON, LAT), P(None, LON, LAT), P(None, LON, LAT), P(LON, LAT), P())
    return jax.shard_map(
        local,
        mesh=split,
        in_specs=placed,
        out_specs=(P(None, None, LAT), P(None, None, LAT), P(None, None, LAT), P(), P(), P()),
        check_vma=False,
    )
```

profile of v0, /device:TPU:8, one launch (start us, length us, event | category | flops | bytes accessed | tf_op | source)
XLA Modules:
  0.0 130.4 jit_solution(12620161045907325382)
XLA Ops:
  0.6 1.3 fusion.10
  1.9 0.6 compare_convert_fusion
  2.6 1.9 %copy.26 = f32[69,45,128]{2,1,0:T(8,128)S(1)} copy(f32[69,45,128]{2,0,1:T(8,128)} %param.7) | data formatting | bytes 3179520 | tf_op args[2]
  4.6 0.5 copy-done.2
  5.0 0.3 fusion.3
  5.4 0.3 copy.27
  5.7 2.2 %copy-done.1 = f32[4,69,45,128]{3,0,2,1:T(4,128)S(1)} copy-done((f32[4,69,45,128]{3,0,2,1:T(4,128)S(1)}, f32[4,69,45,128]{3,0,2,1:T(4,128)}, u32[]{:S(2)}) %copy-start.1) | copy-done | bytes 6359064
  7.8 10.2 %fusion.1 = (f32[4,69,128]{2,0,1:T(4,128)S(1)}, f32[4,69,128]{2,0,1:T(4,128)S(1)}, f32[4,69,128]{2,0,1:T(4,128)S(1)}, f32[4,69,128]{2,0,1:T(4,128)S(1)}) fusion(f32[4,69,45,128]{3,0,2,1:T(4,128)S(1)} %copy-done.1, f32[69,45,128]{2,1,0:T(8,128)S(1)} %copy.27, f32[69,45,128]{2,1,0:T(8,128)S(1)} %copy.26, f32[45,128]{1,0:T(8,128)S(1)} %convert_multiply_fusion), kind=kLoop, calls=%fused_computation.5 | loop fusion | flops 17346048 | bytes 10126848 | tf_op jit(solution)/shard_map/reduce_sum | solution.py:102
  18.0 0.2 copy.28
  18.2 0.2 concatenate.19
  18.4 0.2 copy.29
  18.6 0.2 concatenate.20
  18.8 0.2 copy.30
  19.0 0.2 concatenate.21
  19.2 0.2 copy.31
  19.4 0.2 concatenate.22
  19.6 0.1 copy.32
  19.7 1.5 %concatenate.24 = f32[1173,32,4]{0,2,1:T(4,128)} concatenate(f32[276,32,4]{0,2,1:T(4,128)S(1)} %concatenate.19, f32[276,32,4]{0,2,1:T(4,128)S(1)} %concatenate.20, f32[276,32,4]{0,2,1:T(4,128)S(1)} %concatenate.21, f32[276,32,4]{0,2,1:T(4,128)S(1)} %concatenate.22, f32[69,32,4]{0,2,1:T(4,128)S(1)} %bitcast.36), dimensions={0} | concatenate | bytes 1201152 | tf_op jit(solution)/shard_map/concatenate | solution.py:96
  21.2 11.7 %all-to-all-start = ((f32[32,1173,4]{1,2,0:T(4,128)}), f32[32,1173,4]{1,2,0:T(4,128)S(1)}, u32[]{:S(2)}, u32[]{:S(2)}) async-start(f32[32,1173,4]{1,2,0:T(4,128)} %bitcast.1), calls=%async_computation | async-start | bytes 1310720 | tf_op jit(solution)/shard_map/all_to_all | solution.py:27
  33.0 0.7 concatenate.26
  33.7 0.6 sine_reduce_fusion
  34.4 2.0 %compare_select_fusion.2 = f32[128]{0:T(128)S(1)} fusion(f32[]{:T(128)} %sine_reduce_fusion, s32[]{:T(128)} %get-tuple-element.22, s32[]{:T(128)} %get-tuple-element.23), kind=kLoop, calls=%fused_computation.31 | loop fusion | flops 896 | bytes 524 | tf_op jit(solution)/shard_map/jit(_where)/select_n | solution.py:87
  36.3 0.2 multiply_reduce_fusion.1
  36.6 10.6 %psum.28 = f32[1173]{0:T(1024)S(1)} all-reduce(f32[1173]{0:T(1024)S(1)} %multiply_reduce_fusion.1), channel_id=1, replica_groups=mesh['lat_0'=4,'lat_1'=2,'lon_0'=4,'lon_1'=8] {'lat_0'}, use_global_device_ids=true, to_apply=%region_10.11 | all-reduce | flops 1173 | bytes 9384 | tf_op jit(solution)/shard_map/psum | solution.py:16
  47.2 2.5 %psum.29 = f32[1173]{0:T(1024)S(1)} all-reduce(f32[1173]{0:T(1024)S(1)} %psum.28), channel_id=1, replica_groups=mesh['lat_0'=4,'lat_1'=2,'lon_0'=4,'lon_1'=8] {'lat_1'}, use_global_device_ids=true, to_apply=%region_11.12 | all-reduce | flops 1173 | bytes 9384 | tf_op jit(solution)/shard_map/psum | solution.py:16
  49.7 8.7 %psum.30 = f32[1173]{0:T(1024)S(1)} all-reduce(f32[1173]{0:T(1024)S(1)} %psum.29), channel_id=1, replica_groups=mesh['lat_0'=4,'lat_1'=2,'lon_0'=4,'lon_1'=8] {'lon_0'}, use_global_device_ids=true, to_apply=%region_12.13 | all-reduce | flops 1173 | bytes 9384 | tf_op jit(solution)/shard_map/psum | solution.py:16
  58.4 17.1 %psum.31 = f32[1173]{0:T(1024)S(1)} all-reduce(f32[1173]{0:T(1024)S(1)} %psum.30), channel_id=1, replica_groups=mesh['lat_0'=4,'lat_1'=2,'lon_0'=4,'lon_1'=8] {'lon_1'}, use_global_device_ids=true, to_apply=%region_13.14 | all-reduce | flops 1173 | bytes 9384 | tf_op jit(solution)/shard_map/psum | solution.py:16
  75.6 0.1 div.94
  75.8 0.7 div.92
  76.4 0.7 sqrt.14
  77.2 0.6 rsqrt_multiply_fusion
  77.8 0.1 reduce_sum.96
  78.0 0.1 div.79
  78.2 0.1 reshape.183
  78.3 0.1 div.75
  78.4 0.1 reshape.181
  78.5 0.1 div.77
  78.5 0.1 reshape.182
  78.6 0.1 maximum_bitcast_fusion
  78.7 48.9 %all-gather = f32[32,4,828]{2,1,0:T(4,128)S(1)} all-gather(f32[1,4,828]{2,1,0:T(4,128)S(1)} %maximum_bitcast_fusion), channel_id=1, replica_groups=mesh['lat_0'=4,'lat_1'=2,'lon_0'=4,'lon_1'=8] {'lon_0','lon_1'}, dimensions={0}, use_global_device_ids=true | all-gather | bytes 437184 | tf_op jit(solution)/shard_map/all_gather | solution.py:34
  127.6 0.2 reshape.192
  127.7 0.2 fusion.12
  127.9 0.1 copy.33
  128.0 0.7 copy.40
  128.7 0.1 copy.34
  128.8 0.7 copy.41
  129.5 0.1 copy.35
  129.7 0.7 copy.42
  (26 shorter events, 0.6 us)
Async XLA Ops:
  0.6 3.9 %copy-start.3 = (s32[45,128]{1,0:T(8,128)S(1)}, s32[45,128]{1,0:T(8,128)}, u32[]{:S(2)}) copy-start(s32[45,128]{1,0:T(8,128)} %param.8) | copy-start | bytes 69124
  2.6 2.0 %copy-start = (f32[69,45,128]{2,0,1:T(8,128)S(1)}, f32[69,45,128]{2,0,1:T(8,128)}, u32[]{:S(2)}) copy-start(f32[69,45,128]{2,0,1:T(8,128)} %param.7) | copy-start | bytes 4769284
  2.6 2.4 %copy-start.2 = (f32[69,45,128]{2,0,1:T(8,128)S(1)}, f32[69,45,128]{2,0,1:T(8,128)}, u32[]{:S(2)}) copy-start(f32[69,45,128]{2,0,1:T(8,128)} %param.6) | copy-start | bytes 4769284
  5.0 2.8 %copy-start.1 = (f32[4,69,45,128]{3,0,2,1:T(4,128)S(1)}, f32[4,69,45,128]{3,0,2,1:T(4,128)}, u32[]{:S(2)}) copy-start(f32[4,69,45,128]{3,0,2,1:T(4,128)} %param.5) | copy-start | bytes 19077124
  21.2 56.6 %all-to-all-start = ((f32[32,1173,4]{1,2,0:T(4,128)}), f32[32,1173,4]{1,2,0:T(4,128)S(1)}, u32[]{:S(2)}, u32[]{:S(2)}) async-start(f32[32,1173,4]{1,2,0:T(4,128)} %bitcast.1), calls=%async_computation | async-start | bytes 1310720 | tf_op jit(solution)/shard_map/all_to_all | solution.py:27
where the time goes:
time: 131 us; the launch traced here: 130 us
  blocking collectives  87.7 us (67%)
  other arithmetic  16.4 us (13%)
  local copies, waits for them, and re-layouts  13.6 us (10%)
  starting transfers between devices  11.7 us (9%)
    all_gather x1, blocking collectives, gather_turned(): filled, at, done = (lax.all_gather(both, axis, axis=0, tiled=True), 0, [])  48.9 us
    psum x4, blocking collectives, by_axis(): return functools.reduce(lax.psum, axes, shard)  38.9 us
    all_to_all x1, starting transfers between devices, sent_and_summed(): lax.all_to_all(split_up(shard, dim, devices), axis, 0, 0, tiled=True)  11.7 us
    reduce_sum x1, other arithmetic, local(): jnp.sum(retained_entries * predicted_anomaly * observed_anomaly[None], ax...  10.2 us
    unnamed x13, local copies, waits for them, and re-layouts  6.8 us
    concatenate x6, local copies, waits for them, and re-layouts, local(): jnp.concatenate([jnp.sum(retained_entries * mistake_field * mistake_field...  3.03 us
  transfers between devices with their start and end apart: 1, of which 0 were waited for; matrix products, arithmetic and copies ran while one was open for 5% of the time, Pallas kernels for 0%

commit v1 on v0

--- a/solution.py
+++ b/solution.py
@@ -31,7 +31,13 @@
 def gather_turned(arrays, axis, dims):
     turned = [jnp.moveaxis(a, dim, 0) for a, dim in zip(arrays, dims)]
     both = jnp.concatenate([t.reshape(len(t), -1) for t in turned], axis=1)
-    filled, at, done = (lax.all_gather(both, axis, axis=0, tiled=True), 0, [])
+    filled, at, done = (
+        jnp.concatenate(
+            lax.all_to_all(jnp.stack([both] * lax.axis_size(axis)), axis, 0, 0), axis=0
+        ),
+        0,
+        [],
+    )
     for t, dim in zip(turned, dims):
         slab = filled[:, at : at + t[0].size].reshape(-1, *t.shape[1:])
         done.append(jnp.moveaxis(slab, 0, dim))

time: 131 us -> 105 us (0.80)
  blocking collectives: 87.7 us -> 38.9 us
  waiting for transfers between devices: 0.01 us -> 14.5 us
  starting transfers between devices: 11.7 us -> 19 us
    all_gather x1 -> x0, blocking collectives: 48.9 us -> none  [gather_turned(): filled, at, done = (lax.all_gather(both, axis, axis=0, tiled=True), 0, [])]
    all_to_all x1, waiting for transfers between devices: 0.01 us -> 14.5 us  [sent_and_summed(): lax.all_to_all(split_up(shard, dim, devices), axis, 0, 0, tiled=True)]
    all_to_all x0 -> x1, starting transfers between devices: none -> 7.31 us  [gather_turned(): lax.all_to_all(jnp.stack([both] * lax.axis_size(axis)), axis, 0, 0)]
    unnamed x13 -> x12, local copies, waits for them, and re-layouts: 6.8 us -> 6.64 us
  transfers between devices with their start and end apart: 1 -> 2, of which waited for: 0 -> 1; matrix products, arithmetic and copies ran while one was open for 5% -> 6% of each run, Pallas kernels for 0% -> 0%
where the time goes in v1:
time: 105 us; the launch traced here: 104 us
  blocking collectives  38.9 us (37%)
  starting transfers between devices  19 us (18%)
  other arithmetic  16.4 us (16%)
  waiting for transfers between devices  14.5 us (14%)
  local copies, waits for them, and re-layouts  14.4 us (14%)
    psum x4, blocking collectives, by_axis(): return functools.reduce(lax.psum, axes, shard)  38.9 us
    all_to_all x1, waiting for transfers between devices, sent_and_summed(): lax.all_to_all(split_up(shard, dim, devices), axis, 0, 0, tiled=True)  14.5 us
    all_to_all x1, starting transfers between devices, sent_and_summed(): lax.all_to_all(split_up(shard, dim, devices), axis, 0, 0, tiled=True)  11.7 us
    reduce_sum x1, other arithmetic, local(): jnp.sum(retained_entries * predicted_anomaly * observed_anomaly[None], ax...  10.2 us
    all_to_all x1, starting transfers between devices, gather_turned(): lax.all_to_all(jnp.stack([both] * lax.axis_size(axis)), axis, 0, 0)  7.31 us
    unnamed x12, local copies, waits for them, and re-layouts  6.64 us
    concatenate x6, local copies, waits for them, and re-layouts, local(): jnp.concatenate([jnp.sum(retained_entries * mistake_field * mistake_field...  3.03 us
  transfers between devices with their start and end apart: 2, of which 1 were waited for; matrix products, arithmetic and copies ran while one was open for 6% of the time, Pallas kernels for 0%

profile of v1, /device:TPU:8, one launch (start us, length us, event | category | flops | bytes accessed | tf_op | source)
XLA Modules:
  0.0 104.2 jit_solution(1039098703170629257)
XLA Ops:
  0.6 1.3 %fusion.10 = (s32[]{:T(128)}, s32[]{:T(128)}) fusion(s32[8]{0:T(128)} %param.9, s32[]{:T(128)S(6)} %add.21), kind=kLoop, calls=%fused_computation.34 | loop fusion | flops 46 | bytes 44 | tf_op jit(solution)/shard_map/reduce_sum | solution.py:86
  1.9 0.6 compare_convert_fusion
  2.6 1.9 %copy.27 = f32[69,45,128]{2,1,0:T(8,128)S(1)} copy(f32[69,45,128]{2,0,1:T(8,128)} %param.7) | data formatting | bytes 3179520 | tf_op args[2]
  4.6 0.5 copy-done.2
  5.0 0.3 fusion.3
  5.4 0.3 copy.28
  5.7 2.2 %copy-done.1 = f32[4,69,45,128]{3,0,2,1:T(4,128)S(1)} copy-done((f32[4,69,45,128]{3,0,2,1:T(4,128)S(1)}, f32[4,69,45,128]{3,0,2,1:T(4,128)}, u32[]{:S(2)}) %copy-start.1) | copy-done | bytes 6359064
  7.8 10.2 %fusion.1 = (f32[4,69,128]{2,0,1:T(4,128)S(1)}, f32[4,69,128]{2,0,1:T(4,128)S(1)}, f32[4,69,128]{2,0,1:T(4,128)S(1)}, f32[4,69,128]{2,0,1:T(4,128)S(1)}) fusion(f32[4,69,45,128]{3,0,2,1:T(4,128)S(1)} %copy-done.1, f32[69,45,128]{2,1,0:T(8,128)S(1)} %copy.28, f32[69,45,128]{2,1,0:T(8,128)S(1)} %copy.27, f32[45,128]{1,0:T(8,128)S(1)} %convert_multiply_fusion), kind=kLoop, calls=%fused_computation.5 | loop fusion | flops 17346048 | bytes 10126848 | tf_op jit(solution)/shard_map/reduce_sum | solution.py:108
  18.0 0.2 copy.29
  18.2 0.2 concatenate.19
  18.4 0.2 copy.30
  18.6 0.2 concatenate.20
  18.8 0.2 copy.31
  19.0 0.2 concatenate.21
  19.2 0.2 copy.32
  19.4 0.2 concatenate.22
  19.6 0.1 copy.33
  19.7 1.5 %concatenate.24 = f32[1173,32,4]{0,2,1:T(4,128)} concatenate(f32[276,32,4]{0,2,1:T(4,128)S(1)} %concatenate.19, f32[276,32,4]{0,2,1:T(4,128)S(1)} %concatenate.20, f32[276,32,4]{0,2,1:T(4,128)S(1)} %concatenate.21, f32[276,32,4]{0,2,1:T(4,128)S(1)} %concatenate.22, f32[69,32,4]{0,2,1:T(4,128)S(1)} %bitcast.34), dimensions={0} | concatenate | bytes 1201152 | tf_op jit(solution)/shard_map/concatenate | solution.py:102
  21.2 11.7 %all-to-all-start = ((f32[32,1173,4]{1,2,0:T(4,128)}), f32[32,1173,4]{1,2,0:T(4,128)S(1)}, u32[]{:S(2)}, u32[]{:S(2)}) async-start(f32[32,1173,4]{1,2,0:T(4,128)} %bitcast.1), calls=%async_computation | async-start | bytes 1310720 | tf_op jit(solution)/shard_map/all_to_all | solution.py:27
  33.0 0.7 concatenate.26
  33.7 0.6 sine_reduce_fusion
  34.4 2.0 %compare_select_fusion.2 = f32[128]{0:T(128)S(1)} fusion(f32[]{:T(128)} %sine_reduce_fusion, s32[]{:T(128)} %get-tuple-element.22, s32[]{:T(128)} %get-tuple-element.23), kind=kLoop, calls=%fused_computation.31 | loop fusion | flops 896 | bytes 524 | tf_op jit(solution)/shard_map/jit(_where)/select_n | solution.py:93
  36.3 14.5 %all-to-all-done = f32[32,1173,4]{1,2,0:T(4,128)S(1)} async-done(((f32[32,1173,4]{1,2,0:T(4,128)}), f32[32,1173,4]{1,2,0:T(4,128)S(1)}, u32[]{:S(2)}, u32[]{:S(2)}) %all-to-all-start) | async-done | bytes 600608 | tf_op jit(solution)/shard_map/all_to_all | solution.py:27
  50.9 0.1 reduce_sum.96
  51.1 0.1 div.79
  51.2 0.1 max.42
  51.3 0.1 reshape.188
  51.5 0.1 reshape.186
  51.6 0.1 reshape.187
  51.8 0.8 stack.2
  52.7 7.3 %all-to-all-start.1 = ((f32[32,4,828]{2,1,0:T(4,128)}), f32[32,4,828]{2,1,0:T(4,128)S(1)}, u32[]{:S(2)}, u32[]{:S(2)}) async-start(f32[32,4,828]{2,1,0:T(4,128)} %stack.2), calls=%async_computation.1 | async-start | bytes 917504 | tf_op jit(solution)/shard_map/all_to_all | solution.py:36
  60.0 0.2 multiply_reduce_fusion.1
  60.2 10.6 %psum.28 = f32[1173]{0:T(1024)S(1)} all-reduce(f32[1173]{0:T(1024)S(1)} %multiply_reduce_fusion.1), channel_id=1, replica_groups=mesh['lat_0'=4,'lat_1'=2,'lon_0'=4,'lon_1'=8] {'lat_0'}, use_global_device_ids=true, to_apply=%region_10.11 | all-reduce | flops 1173 | bytes 9384 | tf_op jit(solution)/shard_map/psum | solution.py:16
  70.8 2.5 %psum.29 = f32[1173]{0:T(1024)S(1)} all-reduce(f32[1173]{0:T(1024)S(1)} %psum.28), channel_id=1, replica_groups=mesh['lat_0'=4,'lat_1'=2,'lon_0'=4,'lon_1'=8] {'lat_1'}, use_global_device_ids=true, to_apply=%region_11.12 | all-reduce | flops 1173 | bytes 9384 | tf_op jit(solution)/shard_map/psum | solution.py:16
  73.3 8.7 %psum.30 = f32[1173]{0:T(1024)S(1)} all-reduce(f32[1173]{0:T(1024)S(1)} %psum.29), channel_id=1, replica_groups=mesh['lat_0'=4,'lat_1'=2,'lon_0'=4,'lon_1'=8] {'lon_0'}, use_global_device_ids=true, to_apply=%region_12.13 | all-reduce | flops 1173 | bytes 9384 | tf_op jit(solution)/shard_map/psum | solution.py:16
  82.0 17.1 %psum.31 = f32[1173]{0:T(1024)S(1)} all-reduce(f32[1173]{0:T(1024)S(1)} %psum.30), channel_id=1, replica_groups=mesh['lat_0'=4,'lat_1'=2,'lon_0'=4,'lon_1'=8] {'lon_1'}, use_global_device_ids=true, to_apply=%region_13.14 | all-reduce | flops 1173 | bytes 9384 | tf_op jit(solution)/shard_map/psum | solution.py:16
  99.2 0.1 div.94
  99.4 0.7 div.92
  100.1 0.7 sqrt.14
  100.8 0.6 rsqrt_multiply_fusion
  101.4 0.2 reshape.189
  101.5 0.2 fusion.12
  101.7 0.1 copy.34
  101.8 0.7 copy.41
  102.5 0.1 copy.35
  102.7 0.7 copy.42
  103.4 0.1 copy.36
  103.5 0.7 copy.43
  (28 shorter events, 0.8 us)
Async XLA Ops:
  0.6 3.9 %copy-start.3 = (s32[45,128]{1,0:T(8,128)S(1)}, s32[45,128]{1,0:T(8,128)}, u32[]{:S(2)}) copy-start(s32[45,128]{1,0:T(8,128)} %param.8) | copy-start | bytes 69124
  2.6 2.0 %copy-start = (f32[69,45,128]{2,0,1:T(8,128)S(1)}, f32[69,45,128]{2,0,1:T(8,128)}, u32[]{:S(2)}) copy-start(f32[69,45,128]{2,0,1:T(8,128)} %param.7) | copy-start | bytes 4769284
  2.6 2.4 %copy-start.2 = (f32[69,45,128]{2,0,1:T(8,128)S(1)}, f32[69,45,128]{2,0,1:T(8,128)}, u32[]{:S(2)}) copy-start(f32[69,45,128]{2,0,1:T(8,128)} %param.6) | copy-start | bytes 4769284
  5.0 2.8 %copy-start.1 = (f32[4,69,45,128]{3,0,2,1:T(4,128)S(1)}, f32[4,69,45,128]{3,0,2,1:T(4,128)}, u32[]{:S(2)}) copy-start(f32[4,69,45,128]{3,0,2,1:T(4,128)} %param.5) | copy-start | bytes 19077124
  21.2 29.7 %all-to-all-start = ((f32[32,1173,4]{1,2,0:T(4,128)}), f32[32,1173,4]{1,2,0:T(4,128)S(1)}, u32[]{:S(2)}, u32[]{:S(2)}) async-start(f32[32,1173,4]{1,2,0:T(4,128)} %bitcast.1), calls=%async_computation | async-start | bytes 1310720 | tf_op jit(solution)/shard_map/all_to_all | solution.py:27
  52.7 48.7 %all-to-all-start.1 = ((f32[32,4,828]{2,1,0:T(4,128)}), f32[32,4,828]{2,1,0:T(4,128)S(1)}, u32[]{:S(2)}, u32[]{:S(2)}) async-start(f32[32,4,828]{2,1,0:T(4,128)} %stack.2), calls=%async_computation.1 | async-start | bytes 917504 | tf_op jit(solution)/shard_map/all_to_all | solution.py:36
